TPU v7x, 32 devices: a whole 2x2x4 slice. The times are simulated.
32 devices in a mesh: slab: 8 (over y, x, core), det: 4 (over z).
Axes of the slice: x: 2, y: 2, z: 4, core: 2. Of those that a mesh axis runs over, the one named last changes fastest.
Arguments:
- traces: float32 [32, 128, 4096], P(('slab', 'det')), may hold values from -6 to 6
- tables: bfloat16 [32, 256, 2048], P('slab', None, 'det'), may hold values from -0.0625 to 0.0625
- slab_range: int32 [32, 2], P(('slab', 'det')), may hold values from 0 to 7, as said below
- table_slot: int32 [32, 7], P(('slab', 'det')), may hold values from 0 to 3
- sample_start: int32 [32, 7], P(('slab', 'det')), may hold values from 0 to 3840
Outputs:
- image: float32 [128, 16384], P(None, ('slab', 'det'))
Inputs may be any that keep to these rules, and one draw needn't show every extreme that they name: For detector d with home slab g = d // 4: max(0, g - 3) <= slab_range[d, 0] <= g <= slab_range[d, 1] <= min(7, g + 3); some detectors reach the full 3 on both sides where the grid allows.
All inputs are finite; a program needn't handle non-finite values.
Results may differ from a plain program's by a relative error of at most 0.007.
Values may be sent and summed in bfloat16 or wider, within the bound.
No kernel may reach another device: no remote copies, remote signals or barrier semaphores. Data moves between devices by JAX's collectives and lax.ppermute only.
A program may use at most 64 MiB of HBM per device.

v0:
```python
import jax
import jax.numpy as jnp
from jax import lax
from jax.sharding import PartitionSpec as P

KWIN = 256
NTAB = 4
RANGE = 3


def shifted(x, axis, by):
    peers = lax.axis_size(axis)
    pairs = [(i, i + by) for i in range(peers) if 0 <= i + by < peers]
    return lax.ppermute(x, axis, pairs)


def cut_windows(trace_rows, starts):

    def single(trace_row, first_index):
        return lax.dynamic_slice_in_dim(trace_row, first_index, KWIN, 1)

    return jax.vmap(single)(trace_rows, starts)


def bin_windows(windows, slot_ids, active):
    onehot = (slot_ids[:, None] == jnp.arange(NTAB, dtype=jnp.int32)[None, :]) & active[:, None]
    onehot = onehot.astype(jnp.bfloat16)
    return jnp.einsum("it,ifk->tfk", onehot, windows, preferred_element_type=jnp.float32)


def body(traces, tables, slab_range, table_slot, sample_start):
    position = lax.axis_index("slab")
    samples = traces.astype(jnp.bfloat16)
    own_active = (slab_range[:, 0] <= position) & (position <= slab_range[:, 1])
    stacked = bin_windows(
        cut_windows(samples, sample_start[:, RANGE]), table_slot[:, RANGE], own_active
    )
    for offset in list(range(-RANGE, 0)) + list(range(1, RANGE + 1)):
        target = position + offset
        active = (slab_range[:, 0] <= target) & (target <= slab_range[:, 1])
        windows = cut_windows(samples, sample_start[:, offset + RANGE])
        windows = windows * active[:, None, None].astype(jnp.bfloat16)
        arrived_windows, arrived_slots = shifted(
            (windows, table_slot[:, offset + RANGE]), "slab", offset
        )
        everything = jnp.ones(arrived_slots.shape, jnp.bool_)
        stacked = stacked + bin_windows(arrived_windows, arrived_slots, everything)
    binned = stacked.astype(jnp.bfloat16)
    partial_image = jnp.einsum(
        "tfk,tkv->fv",
        binned,
        lax.all_gather(tables, "det", axis=2, tiled=True),
        preferred_element_type=jnp.float32,
    )
    return lax.psum_scatter(partial_image, "det", scatter_dimension=1, tiled=True)


def solution(mesh):
    placed = (
        P(("slab", "det"), None, None),
        P("slab", None, "det"),
        P(("slab", "det"), None),
        P(("slab", "det"), None),
        P(("slab", "det"), None),
    )
    return jax.shard_map(
        body, mesh=mesh, in_specs=placed, out_specs=P(None, ("slab", "det")), check_vma=False
    )
```

profile of v0, /device:TPU:0, one launch (start us, length us, event | category | flops | bytes accessed | tf_op | source)
XLA Modules:
  0.0 129.3 jit_solution(1520195266104620349)
XLA Ops:
  6.5 0.0 all-gather.2.cloned.1.call-start
  6.5 0.7 all-gather.2.cloned.1.call-update
  7.3 0.0 reduce-scatter.2.cloned.1.call-start
  7.3 1.6 %fusion.21 = (s32[1,1]{1,0:T(1,128)}, s32[1,1]{1,0:T(1,128)}, s32[1,1]{1,0:T(1,128)}, s32[1,1]{1,0:T(1,128)}, s32[1,1]{1,0:T(1,128)}, /*index=5*/s32[1,1]{1,0:T(1,128)}, s32[1,1]{1,0:T(1,128)}) fusion(s32[1,7]{1,0:T(1,128)} %param.8), kind=kLoop, calls=%fused_computation.43 | loop fusion | bytes 56 | tf_op jit(solution)/shard_map/slice | solution.py:36
  8.9 3.0 %collective-permute-start.6 = (s32[1]{0:T(128)}, s32[1]{0:T(128)}, u32[]{:S(2)}, u32[]{:S(2)}) collective-permute-start(s32[1]{0:T(128)} %bitcast.33), channel_id=1, source_target_pairs={{0,4},{4,8},{8,12},{12,16},{16,20},{20,24},{24,28},{1,5},{5,9},{9,... | collective-permute-start | bytes 20 | tf_op jit(solution)/shard_map/ppermute | solution.py:14
  11.9 1.3 collective-permute-start.4
  13.1 1.3 collective-permute-start.2
  14.4 1.3 collective-permute-start
  15.7 7.7 %collective-permute-start.10 = (s32[1]{0:T(128)}, s32[1]{0:T(128)}, u32[]{:S(2)}, u32[]{:S(2)}) collective-permute-start(s32[1]{0:T(128)} %bitcast.49), channel_id=1, source_target_pairs={{0,12},{4,16},{8,20},{12,24},{16,28},{1,13},{5,17},{9,21},{13,25},... | collective-permute-start | bytes 20 | tf_op jit(solution)/shard_map/ppermute | solution.py:14
  23.4 1.3 %fusion.23 = (s32[1,1]{1,0:T(1,128)}, s32[1,1]{1,0:T(1,128)}) fusion(s32[1,2]{1,0:T(1,128)} %param.7), kind=kLoop, calls=%fused_computation.45 | loop fusion | bytes 16 | tf_op jit(solution)/shard_map/slice | solution.py:34
  33.7 1.6 %fusion.22 = (s32[1,1]{1,0:T(1,128)}, s32[1,1]{1,0:T(1,128)}, s32[1,1]{1,0:T(1,128)}, s32[1,1]{1,0:T(1,128)}, s32[1,1]{1,0:T(1,128)}, /*index=5*/s32[1,1]{1,0:T(1,128)}, s32[1,1]{1,0:T(1,128)}) fusion(s32[1,7]{1,0:T(1,128)} %param.9), kind=kLoop, calls=%fused_computation.44 | loop fusion | bytes 56 | tf_op jit(solution)/shard_map/slice | solution.py:36
  44.2 1.7 %convert_element_type.10 = bf16[1,128,4096]{2,1,0:T(8,128)(2,1)S(1)} convert(f32[1,128,4096]{2,1,0:T(8,128)} %param.5) | non-fusion elementwise | flops 524288 | bytes 3145728 | tf_op jit(solution)/shard_map/convert_element_type | solution.py:33
  50.4 0.6 fusion.14
  51.0 0.2 bitcast_convert_fusion.6
  51.2 0.0 collective-permute-done.6
  51.2 5.9 %collective-permute-start.8 = (s32[1]{0:T(128)}, s32[1]{0:T(128)}, u32[]{:S(2)}, u32[]{:S(2)}) collective-permute-start(s32[1]{0:T(128)} %bitcast.41), channel_id=1, source_target_pairs={{0,8},{4,12},{8,16},{12,20},{16,24},{20,28},{1,9},{5,13},{9,17},{1... | collective-permute-start | bytes 20 | tf_op jit(solution)/shard_map/ppermute | solution.py:14
  57.1 0.7 fusion.18
  57.8 0.0 collective-permute-done.4
  57.8 1.3 %collective-permute-start.11 = (bf16[1,128,256]{2,1,0:T(8,128)(2,1)S(1)}, bf16[1,128,256]{2,1,0:T(8,128)(2,1)S(1)}, u32[]{:S(2)}, u32[]{:S(2)}) collective-permute-start(bf16[1,128,256]{2,1,0:T(8,128)(2,1)S(1)} %get-tuple-element.83), channel_id=1, source_target_pairs={{0,12},{4,16},{8,20},{12,24},{16,28},{1,13},{5,17},{9,21},{13,25},... | collective-permute-start | bytes 196616 | tf_op jit(solution)/shard_map/ppermute | solution.py:14
  59.1 0.6 fusion.17
  59.8 0.0 collective-permute-done.2
  59.8 2.9 %collective-permute-start.9 = (bf16[1,128,256]{2,1,0:T(8,128)(2,1)S(1)}, bf16[1,128,256]{2,1,0:T(8,128)(2,1)S(1)}, u32[]{:S(2)}, u32[]{:S(2)}) collective-permute-start(bf16[1,128,256]{2,1,0:T(8,128)(2,1)S(1)} %get-tuple-element.84), channel_id=1, source_target_pairs={{0,8},{4,12},{8,16},{12,20},{16,24},{20,28},{1,9},{5,13},{9,17},{1... | collective-permute-start | bytes 196616 | tf_op jit(solution)/shard_map/ppermute | solution.py:14
  62.6 0.6 fusion.16
  63.3 0.0 collective-permute-done
  63.3 1.3 %collective-permute-start.7 = (bf16[1,128,256]{2,1,0:T(8,128)(2,1)S(1)}, bf16[1,128,256]{2,1,0:T(8,128)(2,1)S(1)}, u32[]{:S(2)}, u32[]{:S(2)}) collective-permute-start(bf16[1,128,256]{2,1,0:T(8,128)(2,1)S(1)} %get-tuple-element.85), channel_id=1, source_target_pairs={{0,4},{4,8},{8,12},{12,16},{16,20},{20,24},{24,28},{1,5},{5,9},{9,... | collective-permute-start | bytes 196616 | tf_op jit(solution)/shard_map/ppermute | solution.py:14
  64.6 0.6 fusion.15
  65.2 0.0 collective-permute-done.10
  65.3 1.3 collective-permute-start.5
  66.6 0.6 fusion.20
  67.2 0.0 collective-permute-done.8
  67.2 1.3 collective-permute-start.3
  68.5 0.7 fusion.19
  69.2 0.0 collective-permute-done.11
  69.2 1.3 collective-permute-start.1
  70.5 0.0 collective-permute-done.9
  70.5 0.0 collective-permute-done.7
  70.6 0.0 collective-permute-done.5
  70.6 4.5 %collective-permute-done.3 = bf16[1,128,256]{2,1,0:T(8,128)(2,1)S(1)} collective-permute-done((bf16[1,128,256]{2,1,0:T(8,128)(2,1)S(1)}, bf16[1,128,256]{2,1,0:T(8,128)(2,1)S(1)}, u32[]{:S(2)}, u32[]{:S(2)}) %collective-permute-start.3) | collective-permute-done | bytes 65568 | tf_op jit(solution)/shard_map/ppermute | solution.py:14
  75.1 1.9 %collective-permute-done.1 = bf16[1,128,256]{2,1,0:T(8,128)(2,1)S(1)} collective-permute-done((bf16[1,128,256]{2,1,0:T(8,128)(2,1)S(1)}, bf16[1,128,256]{2,1,0:T(8,128)(2,1)S(1)}, u32[]{:S(2)}, u32[]{:S(2)}) %collective-permute-start.1) | collective-permute-done | bytes 65568 | tf_op jit(solution)/shard_map/ppermute | solution.py:14
  77.0 15.4 %all-gather.2.cloned.1.call-done = bf16[4,256,2048]{2,1,0:T(8,128)(2,1)} async-done(((bf16[4,256,512]{2,1,0:T(8,128)(2,1)}), bf16[4,256,2048]{2,1,0:T(8,128)(2,1)}) %all-gather.2.cloned.1.call-update) | async-done | bytes 4194320 | tf_op jit(solution)/shard_map/all_gather | solution.py:52
  92.4 4.1 %convolution_bitcast_fusion = f32[128,2048]{1,0:T(8,128)} fusion(bf16[4,256,2048]{2,1,0:T(8,128)(2,1)} %all-gather.2.cloned.1.call-done, f32[128,256]{1,0:T(8,128)S(1)} %bitcast_convert_fusion, f32[4]{0:T(128)S(1)} %fusion.20, f32[128,256]{1,0:T(8,128)S(1)} %bitcast_convert_fusion.1, f32[4]{0:T(128)S(1)} %fusion.19, f32[128,256]{1,0:T(8,128)S(1)} %bitcast_convert_fusion.2, ...), kind=kOutput, calls=%fused_computation | convolution fusion | flops 538705920 | bytes 6160496 | tf_op jit(solution)/shard_map/tfk,tkv->fv/dot_general | solution.py:49
  96.5 0.0 reduce-scatter.2.cloned.1.call-update
  96.5 25.9 %reduce-scatter.2.cloned.1.call-done = f32[128,512]{1,0:T(8,128)} async-done(((f32[128,2048]{1,0:T(8,128)}), f32[128,512]{1,0:T(8,128)}) %reduce-scatter.2.cloned.1.call-update) | async-done | bytes 262160 | tf_op jit(solution)/shard_map/reduce_scatter | solution.py:55
  (6 shorter events, 0.1 us)
Async XLA Ops:
  6.5 85.9 %all-gather.2.cloned.1.call-start = ((), (), s32[]{:S(2)}) async-start(), calls=%async_computation.1 | async-start | bytes 5242880 | tf_op jit(solution)/shard_map/all_gather | solution.py:52
  7.3 115.2 %reduce-scatter.2.cloned.1.call-start = ((), (), s32[]{:S(2)}) async-start(), calls=%async_computation.2 | async-start | bytes 1310720 | tf_op jit(solution)/shard_map/reduce_scatter | solution.py:55
  8.9 42.3 %collective-permute-start.6 = (s32[1]{0:T(128)}, s32[1]{0:T(128)}, u32[]{:S(2)}, u32[]{:S(2)}) collective-permute-start(s32[1]{0:T(128)} %bitcast.33), channel_id=1, source_target_pairs={{0,4},{4,8},{8,12},{12,16},{16,20},{20,24},{24,28},{1,5},{5,9},{9,... | collective-permute-start | bytes 20 | tf_op jit(solution)/shard_map/ppermute | solution.py:14
  11.9 46.0 %collective-permute-start.4 = (s32[1]{0:T(128)}, s32[1]{0:T(128)}, u32[]{:S(2)}, u32[]{:S(2)}) collective-permute-start(s32[1]{0:T(128)} %bitcast.25), channel_id=1, source_target_pairs={{4,0},{8,4},{12,8},{16,12},{20,16},{24,20},{28,24},{5,1},{9,5},{13... | collective-permute-start | bytes 20 | tf_op jit(solution)/shard_map/ppermute | solution.py:14
  13.1 46.6 %collective-permute-start.2 = (s32[1]{0:T(128)}, s32[1]{0:T(128)}, u32[]{:S(2)}, u32[]{:S(2)}) collective-permute-start(s32[1]{0:T(128)} %bitcast.17), channel_id=1, source_target_pairs={{8,0},{12,4},{16,8},{20,12},{24,16},{28,20},{9,1},{13,5},{17,9},{2... | collective-permute-start | bytes 20 | tf_op jit(solution)/shard_map/ppermute | solution.py:14
  14.4 48.8 %collective-permute-start = (s32[1]{0:T(128)}, s32[1]{0:T(128)}, u32[]{:S(2)}, u32[]{:S(2)}) collective-permute-start(s32[1]{0:T(128)} %bitcast.9), channel_id=1, source_target_pairs={{12,0},{16,4},{20,8},{24,12},{28,16},{13,1},{17,5},{21,9},{25,13},... | collective-permute-start | bytes 20 | tf_op jit(solution)/shard_map/ppermute | solution.py:14
  15.7 49.5 %collective-permute-start.10 = (s32[1]{0:T(128)}, s32[1]{0:T(128)}, u32[]{:S(2)}, u32[]{:S(2)}) collective-permute-start(s32[1]{0:T(128)} %bitcast.49), channel_id=1, source_target_pairs={{0,12},{4,16},{8,20},{12,24},{16,28},{1,13},{5,17},{9,21},{13,25},... | collective-permute-start | bytes 20 | tf_op jit(solution)/shard_map/ppermute | solution.py:14
  51.2 16.0 %collective-permute-start.8 = (s32[1]{0:T(128)}, s32[1]{0:T(128)}, u32[]{:S(2)}, u32[]{:S(2)}) collective-permute-start(s32[1]{0:T(128)} %bitcast.41), channel_id=1, source_target_pairs={{0,8},{4,12},{8,16},{12,20},{16,24},{20,28},{1,9},{5,13},{9,17},{1... | collective-permute-start | bytes 20 | tf_op jit(solution)/shard_map/ppermute | solution.py:14
  57.8 11.4 %collective-permute-start.11 = (bf16[1,128,256]{2,1,0:T(8,128)(2,1)S(1)}, bf16[1,128,256]{2,1,0:T(8,128)(2,1)S(1)}, u32[]{:S(2)}, u32[]{:S(2)}) collective-permute-start(bf16[1,128,256]{2,1,0:T(8,128)(2,1)S(1)} %get-tuple-element.83), channel_id=1, source_target_pairs={{0,12},{4,16},{8,20},{12,24},{16,28},{1,13},{5,17},{9,21},{13,25},... | collective-permute-start | bytes 196616 | tf_op jit(solution)/shard_map/ppermute | solution.py:14
  59.8 10.7 %collective-permute-start.9 = (bf16[1,128,256]{2,1,0:T(8,128)(2,1)S(1)}, bf16[1,128,256]{2,1,0:T(8,128)(2,1)S(1)}, u32[]{:S(2)}, u32[]{:S(2)}) collective-permute-start(bf16[1,128,256]{2,1,0:T(8,128)(2,1)S(1)} %get-tuple-element.84), channel_id=1, source_target_pairs={{0,8},{4,12},{8,16},{12,20},{16,24},{20,28},{1,9},{5,13},{9,17},{1... | collective-permute-start | bytes 196616 | tf_op jit(solution)/shard_map/ppermute | solution.py:14
  63.3 7.2 %collective-permute-start.7 = (bf16[1,128,256]{2,1,0:T(8,128)(2,1)S(1)}, bf16[1,128,256]{2,1,0:T(8,128)(2,1)S(1)}, u32[]{:S(2)}, u32[]{:S(2)}) collective-permute-start(bf16[1,128,256]{2,1,0:T(8,128)(2,1)S(1)} %get-tuple-element.85), channel_id=1, source_target_pairs={{0,4},{4,8},{8,12},{12,16},{16,20},{20,24},{24,28},{1,5},{5,9},{9,... | collective-permute-start | bytes 196616 | tf_op jit(solution)/shard_map/ppermute | solution.py:14
  65.3 5.3 %collective-permute-start.5 = (bf16[1,128,256]{2,1,0:T(8,128)(2,1)S(1)}, bf16[1,128,256]{2,1,0:T(8,128)(2,1)S(1)}, u32[]{:S(2)}, u32[]{:S(2)}) collective-permute-start(bf16[1,128,256]{2,1,0:T(8,128)(2,1)S(1)} %get-tuple-element.86), channel_id=1, source_target_pairs={{4,0},{8,4},{12,8},{16,12},{20,16},{24,20},{28,24},{5,1},{9,5},{13... | collective-permute-start | bytes 196616 | tf_op jit(solution)/shard_map/ppermute | solution.py:14
  67.2 7.9 %collective-permute-start.3 = (bf16[1,128,256]{2,1,0:T(8,128)(2,1)S(1)}, bf16[1,128,256]{2,1,0:T(8,128)(2,1)S(1)}, u32[]{:S(2)}, u32[]{:S(2)}) collective-permute-start(bf16[1,128,256]{2,1,0:T(8,128)(2,1)S(1)} %get-tuple-element.87), channel_id=1, source_target_pairs={{8,0},{12,4},{16,8},{20,12},{24,16},{28,20},{9,1},{13,5},{17,9},{2... | collective-permute-start | bytes 196616 | tf_op jit(solution)/shard_map/ppermute | solution.py:14
  69.2 7.8 %collective-permute-start.1 = (bf16[1,128,256]{2,1,0:T(8,128)(2,1)S(1)}, bf16[1,128,256]{2,1,0:T(8,128)(2,1)S(1)}, u32[]{:S(2)}, u32[]{:S(2)}) collective-permute-start(bf16[1,128,256]{2,1,0:T(8,128)(2,1)S(1)} %get-tuple-element.88), channel_id=1, source_target_pairs={{12,0},{16,4},{20,8},{24,12},{28,16},{13,1},{17,5},{21,9},{25,13},... | collective-permute-start | bytes 196616 | tf_op jit(solution)/shard_map/ppermute | solution.py:14
Sparse Core Ops, SparseCore 0:
  8.9 83.4 all-gather.1
  96.6 25.7 reduce-scatter.1
where the time goes:
time: 130 us; the launch traced here: 129 us
  waiting for transfers between devices  48.5 us (37%)
  between operations  36 us (28%)
  starting transfers between devices  29.8 us (23%)
  other arithmetic  6.48 us (5%)
  local copies, waits for them, and re-layouts  4.5 us (3%)
  matrix products  4.07 us (3%)
    ppermute x12, starting transfers between devices, shifted(): return lax.ppermute(x, axis, pairs)  29.8 us
    reduce_scatter x1, waiting for transfers between devices, body(): lax.psum_scatter(partial_image, 'det', scatter_dimension=1, tiled=True)  25.9 us
    all_gather x1, waiting for transfers between devices, body(): lax.all_gather(tables, 'det', axis=2, tiled=True)  15.4 us
    ppermute x12, waiting for transfers between devices, shifted(): return lax.ppermute(x, axis, pairs)  6.42 us
    another operation x14, other arithmetic  4.75 us
    dot_general x1, matrix products, body(): jnp.einsum('tfk,tkv->fv', binned, lax.all_gather(tables, 'det', axis=2, t...  4.07 us
  transfers between devices with their start and end apart: 14, of which 4 were waited for; matrix products, arithmetic and copies ran while one was open for 8% of the time, Pallas kernels for 0%

commit v1 on v0

--- a/solution.py
+++ b/solution.py
@@ -49,7 +49,7 @@
     partial_image = jnp.einsum(
         "tfk,tkv->fv",
         binned,
-        lax.all_gather(tables, "det", axis=2, tiled=True),
+        jnp.concatenate(lax.all_gather(tables, "det"), axis=2),
         preferred_element_type=jnp.float32,
     )
     return lax.psum_scatter(partial_image, "det", scatter_dimension=1, tiled=True)

time: 130 us -> 145 us (1.12)
  local copies, waits for them, and re-layouts: 4.5 us -> 18.8 us
  waiting for transfers between devices: 48.5 us -> 53.3 us
  starting transfers between devices: 29.8 us -> 25.2 us
    ppermute x12, waiting for transfers between devices: 6.42 us -> 15.6 us  [shifted(): return lax.ppermute(x, axis, pairs)]
    reshape x0 -> x1, local copies, waits for them, and re-layouts: none -> 7.73 us  [body(): jnp.concatenate(lax.all_gather(tables, 'det'), axis=2)]
    all_gather x0 -> x1, local copies, waits for them, and re-layouts: none -> 7.4 us  [body(): lax.all_gather(tables, 'det')]
    ppermute x12, starting transfers between devices: 29.8 us -> 25.2 us  [shifted(): return lax.ppermute(x, axis, pairs)]
    all_gather x1, waiting for transfers between devices: 15.4 us -> 11 us  [body(): lax.all_gather(tables, 'det')]
  transfers between devices with their start and end apart: 14 -> 14, of which waited for: 4 -> 7; matrix products, arithmetic and copies ran while one was open for 8% -> 7% of each run, Pallas kernels for 0% -> 0%
where the time goes in v1:
time: 145 us; the launch traced here: 144 us
  waiting for transfers between devices  53.3 us (37%)
  between operations  36.5 us (25%)
  starting transfers between devices  25.2 us (17%)
  local copies, waits for them, and re-layouts  18.8 us (13%)
  other arithmetic  6.5 us (4%)
  matrix products  4.08 us (3%)
    reduce_scatter x1, waiting for transfers between devices, body(): lax.psum_scatter(partial_image, 'det', scatter_dimension=1, tiled=True)  25.9 us
    ppermute x12, starting transfers between devices, shifted(): return lax.ppermute(x, axis, pairs)  25.2 us
    ppermute x12, waiting for transfers between devices, shifted(): return lax.ppermute(x, axis, pairs)  15.6 us
    all_gather x1, waiting for transfers between devices, body(): lax.all_gather(tables, 'det')  11 us
    reshape x1, local copies, waits for them, and re-layouts, body(): jnp.concatenate(lax.all_gather(tables, 'det'), axis=2)  7.73 us
    all_gather x1, local copies, waits for them, and re-layouts, body(): lax.all_gather(tables, 'det')  7.4 us
    another operation x14, other arithmetic  4.76 us
    dot_general x1, matrix products, body(): jnp.einsum('tfk,tkv->fv', binned, jnp.concatenate(lax.all_gather(tables,...  4.08 us
  transfers between devices with their start and end apart: 14, of which 7 were waited for; matrix products, arithmetic and copies ran while one was open for 7% of the time, Pallas kernels for 0%

profile of v1, /device:TPU:0, one launch (start us, length us, event | category | flops | bytes accessed | tf_op | source)
XLA Modules:
  0.0 144.4 jit_solution(2626503096963585066)
XLA Ops:
  6.5 0.0 copy-start
  6.5 0.0 all-gather.3.cloned.1.call-start
  6.5 0.7 all-gather.3.cloned.1.call-update
  7.3 0.0 reduce-scatter.2.cloned.1.call-start
  7.3 1.6 %fusion.22 = (s32[1,1]{1,0:T(1,128)}, s32[1,1]{1,0:T(1,128)}, s32[1,1]{1,0:T(1,128)}, s32[1,1]{1,0:T(1,128)}, s32[1,1]{1,0:T(1,128)}, /*index=5*/s32[1,1]{1,0:T(1,128)}, s32[1,1]{1,0:T(1,128)}) fusion(s32[1,7]{1,0:T(1,128)} %param.9), kind=kLoop, calls=%fused_computation.45 | loop fusion | bytes 56 | tf_op jit(solution)/shard_map/slice | solution.py:36
  11.5 1.4 fusion.23
  27.3 1.7 %convert_element_type.10 = bf16[1,128,4096]{2,1,0:T(8,128)(2,1)S(1)} convert(f32[1,128,4096]{2,1,0:T(8,128)} %param.5) | non-fusion elementwise | flops 524288 | bytes 3145728 | tf_op jit(solution)/shard_map/convert_element_type | solution.py:33
  33.5 0.2 bitcast_convert_fusion.6
  33.7 4.3 %collective-permute-start.11 = (bf16[1,128,256]{2,1,0:T(8,128)(2,1)S(1)}, bf16[1,128,256]{2,1,0:T(8,128)(2,1)S(1)}, u32[]{:S(2)}, u32[]{:S(2)}) collective-permute-start(bf16[1,128,256]{2,1,0:T(8,128)(2,1)S(1)} %get-tuple-element.83), channel_id=1, source_target_pairs={{0,12},{4,16},{8,20},{12,24},{16,28},{1,13},{5,17},{9,21},{13,25},... | collective-permute-start | bytes 196616 | tf_op jit(solution)/shard_map/ppermute | solution.py:14
  38.0 0.0 copy-done
  38.1 0.7 fusion.21
  38.7 4.2 %collective-permute-start.10 = (s32[1]{0:T(128)}, s32[1]{0:T(128)}, u32[]{:S(2)}, u32[]{:S(2)}) collective-permute-start(s32[1]{0:T(128)} %bitcast.49), channel_id=1, source_target_pairs={{0,12},{4,16},{8,20},{12,24},{16,28},{1,13},{5,17},{9,21},{13,25},... | collective-permute-start | bytes 20 | tf_op jit(solution)/shard_map/ppermute | solution.py:14
  42.9 1.3 collective-permute-start.9
  44.2 3.8 %collective-permute-start.8 = (s32[1]{0:T(128)}, s32[1]{0:T(128)}, u32[]{:S(2)}, u32[]{:S(2)}) collective-permute-start(s32[1]{0:T(128)} %bitcast.41), channel_id=1, source_target_pairs={{0,8},{4,12},{8,16},{12,20},{16,24},{20,28},{1,9},{5,13},{9,17},{1... | collective-permute-start | bytes 20 | tf_op jit(solution)/shard_map/ppermute | solution.py:14
  48.0 1.3 collective-permute-start.7
  50.7 0.7 fusion.14
  51.4 0.0 collective-permute-done.10
  51.4 2.6 %collective-permute-start.6 = (s32[1]{0:T(128)}, s32[1]{0:T(128)}, u32[]{:S(2)}, u32[]{:S(2)}) collective-permute-start(s32[1]{0:T(128)} %bitcast.33), channel_id=1, source_target_pairs={{0,4},{4,8},{8,12},{12,16},{16,20},{20,24},{24,28},{1,5},{5,9},{9,... | collective-permute-start | bytes 20 | tf_op jit(solution)/shard_map/ppermute | solution.py:14
  54.0 0.6 fusion.20
  54.6 0.0 collective-permute-done.8
  54.6 1.3 collective-permute-start.5
  55.9 0.7 fusion.19
  56.6 0.0 collective-permute-done.6
  56.6 1.3 collective-permute-start.4
  57.9 0.6 fusion.18
  58.5 1.9 %collective-permute-done.4 = s32[1]{0:T(128)} collective-permute-done((s32[1]{0:T(128)}, s32[1]{0:T(128)}, u32[]{:S(2)}, u32[]{:S(2)}) %collective-permute-start.4) | collective-permute-done | bytes 36 | tf_op jit(solution)/shard_map/ppermute | solution.py:14
  60.4 1.3 collective-permute-start.2
  61.7 0.6 fusion.17
  62.4 4.0 %collective-permute-done.2 = s32[1]{0:T(128)} collective-permute-done((s32[1]{0:T(128)}, s32[1]{0:T(128)}, u32[]{:S(2)}, u32[]{:S(2)}) %collective-permute-start.2) | collective-permute-done | bytes 36 | tf_op jit(solution)/shard_map/ppermute | solution.py:14
  66.3 1.3 collective-permute-start
  67.6 0.6 fusion.16
  68.2 3.9 %collective-permute-done = s32[1]{0:T(128)} collective-permute-done((s32[1]{0:T(128)}, s32[1]{0:T(128)}, u32[]{:S(2)}, u32[]{:S(2)}) %collective-permute-start) | collective-permute-done | bytes 36 | tf_op jit(solution)/shard_map/ppermute | solution.py:14
  72.2 1.3 collective-permute-start.3
  73.4 0.7 fusion.15
  74.1 0.0 collective-permute-done.11
  74.1 1.3 collective-permute-start.1
  75.5 0.0 collective-permute-done.9
  75.5 0.0 collective-permute-done.7
  75.5 0.0 collective-permute-done.5
  75.5 3.9 %collective-permute-done.3 = bf16[1,128,256]{2,1,0:T(8,128)(2,1)S(1)} collective-permute-done((bf16[1,128,256]{2,1,0:T(8,128)(2,1)S(1)}, bf16[1,128,256]{2,1,0:T(8,128)(2,1)S(1)}, u32[]{:S(2)}, u32[]{:S(2)}) %collective-permute-start.3) | collective-permute-done | bytes 65568 | tf_op jit(solution)/shard_map/ppermute | solution.py:14
  79.5 1.9 %collective-permute-done.1 = bf16[1,128,256]{2,1,0:T(8,128)(2,1)S(1)} collective-permute-done((bf16[1,128,256]{2,1,0:T(8,128)(2,1)S(1)}, bf16[1,128,256]{2,1,0:T(8,128)(2,1)S(1)}, u32[]{:S(2)}, u32[]{:S(2)}) %collective-permute-start.1) | collective-permute-done | bytes 65568 | tf_op jit(solution)/shard_map/ppermute | solution.py:14
  81.4 11.0 %all-gather.3.cloned.1.call-done = bf16[16,256,512]{2,1,0:T(8,128)(2,1)} async-done(((bf16[4,256,512]{2,1,0:T(8,128)(2,1)}), bf16[16,256,512]{2,1,0:T(8,128)(2,1)}) %all-gather.3.cloned.1.call-update) | async-done | bytes 4194320 | tf_op jit(solution)/shard_map/all_gather | solution.py:52
  92.4 7.4 %copy.9 = bf16[4,4,256,512]{3,0,2,1:T(4,128)(2,1)} copy(bf16[4,4,256,512]{3,2,1,0:T(8,128)(2,1)} %bitcast.86) | data formatting | bytes 8388608 | tf_op jit(solution)/shard_map/all_gather | solution.py:52
  99.8 7.7 %reshape.308 = bf16[4,256,2048]{2,1,0:T(8,128)(2,1)} reshape(bf16[4,256,4,512]{3,2,1,0:T(4,128)(2,1)} %bitcast.85) | data formatting | bytes 8388608 | tf_op jit(solution)/shard_map/reshape | solution.py:52
  107.5 4.1 %convolution_bitcast_fusion = f32[128,2048]{1,0:T(8,128)} fusion(bf16[4,256,2048]{2,1,0:T(8,128)(2,1)} %reshape.308, f32[128,256]{1,0:T(8,128)S(1)} %bitcast_convert_fusion, f32[4]{0:T(128)S(1)} %fusion.20, f32[128,256]{1,0:T(8,128)S(1)} %bitcast_convert_fusion.1, f32[4]{0:T(128)S(1)} %fusion.19, f32[128,256]{1,0:T(8,128)S(1)} %bitcast_convert_fusion.2, ...), kind=kOutput, calls=%fused_computation.1 | convolution fusion | flops 538705920 | bytes 6160496 | tf_op jit(solution)/shard_map/tfk,tkv->fv/dot_general | solution.py:49
  111.6 0.0 reduce-scatter.2.cloned.1.call-update
  111.6 25.9 %reduce-scatter.2.cloned.1.call-done = f32[128,512]{1,0:T(8,128)} async-done(((f32[128,2048]{1,0:T(8,128)}), f32[128,512]{1,0:T(8,128)}) %reduce-scatter.2.cloned.1.call-update) | async-done | bytes 262160 | tf_op jit(solution)/shard_map/reduce_scatter | solution.py:55
  (6 shorter events, 0.1 us)
Async XLA Ops:
  6.5 31.5 %copy-start = (s32[1,7]{1,0:T(1,128)S(1)}, s32[1,7]{1,0:T(1,128)}, u32[]{:S(2)}) copy-start(s32[1,7]{1,0:T(1,128)} %param.8) | copy-start | bytes 88
  6.5 85.9 %all-gather.3.cloned.1.call-start = ((), (), s32[]{:S(2)}) async-start(), calls=%async_computation.2 | async-start | bytes 5242880 | tf_op jit(solution)/shard_map/all_gather | solution.py:52
  7.3 130.3 %reduce-scatter.2.cloned.1.call-start = ((), (), s32[]{:S(2)}) async-start(), calls=%async_computation.1 | async-start | bytes 1310720 | tf_op jit(solution)/shard_map/reduce_scatter | solution.py:55
  33.7 40.4 %collective-permute-start.11 = (bf16[1,128,256]{2,1,0:T(8,128)(2,1)S(1)}, bf16[1,128,256]{2,1,0:T(8,128)(2,1)S(1)}, u32[]{:S(2)}, u32[]{:S(2)}) collective-permute-start(bf16[1,128,256]{2,1,0:T(8,128)(2,1)S(1)} %get-tuple-element.83), channel_id=1, source_target_pairs={{0,12},{4,16},{8,20},{12,24},{16,28},{1,13},{5,17},{9,21},{13,25},... | collective-permute-start | bytes 196616 | tf_op jit(solution)/shard_map/ppermute | solution.py:14
  38.7 12.6 %collective-permute-start.10 = (s32[1]{0:T(128)}, s32[1]{0:T(128)}, u32[]{:S(2)}, u32[]{:S(2)}) collective-permute-start(s32[1]{0:T(128)} %bitcast.49), channel_id=1, source_target_pairs={{0,12},{4,16},{8,20},{12,24},{16,28},{1,13},{5,17},{9,21},{13,25},... | collective-permute-start | bytes 20 | tf_op jit(solution)/shard_map/ppermute | solution.py:14
  42.9 32.5 %collective-permute-start.9 = (bf16[1,128,256]{2,1,0:T(8,128)(2,1)S(1)}, bf16[1,128,256]{2,1,0:T(8,128)(2,1)S(1)}, u32[]{:S(2)}, u32[]{:S(2)}) collective-permute-start(bf16[1,128,256]{2,1,0:T(8,128)(2,1)S(1)} %get-tuple-element.84), channel_id=1, source_target_pairs={{0,8},{4,12},{8,16},{12,20},{16,24},{20,28},{1,9},{5,13},{9,17},{1... | collective-permute-start | bytes 196616 | tf_op jit(solution)/shard_map/ppermute | solution.py:14
  44.2 10.3 %collective-permute-start.8 = (s32[1]{0:T(128)}, s32[1]{0:T(128)}, u32[]{:S(2)}, u32[]{:S(2)}) collective-permute-start(s32[1]{0:T(128)} %bitcast.41), channel_id=1, source_target_pairs={{0,8},{4,12},{8,16},{12,20},{16,24},{20,28},{1,9},{5,13},{9,17},{1... | collective-permute-start | bytes 20 | tf_op jit(solution)/shard_map/ppermute | solution.py:14
  48.0 27.5 %collective-permute-start.7 = (bf16[1,128,256]{2,1,0:T(8,128)(2,1)S(1)}, bf16[1,128,256]{2,1,0:T(8,128)(2,1)S(1)}, u32[]{:S(2)}, u32[]{:S(2)}) collective-permute-start(bf16[1,128,256]{2,1,0:T(8,128)(2,1)S(1)} %get-tuple-element.85), channel_id=1, source_target_pairs={{0,4},{4,8},{8,12},{12,16},{16,20},{20,24},{24,28},{1,5},{5,9},{9,... | collective-permute-start | bytes 196616 | tf_op jit(solution)/shard_map/ppermute | solution.py:14
  51.4 5.2 %collective-permute-start.6 = (s32[1]{0:T(128)}, s32[1]{0:T(128)}, u32[]{:S(2)}, u32[]{:S(2)}) collective-permute-start(s32[1]{0:T(128)} %bitcast.33), channel_id=1, source_target_pairs={{0,4},{4,8},{8,12},{12,16},{16,20},{20,24},{24,28},{1,5},{5,9},{9,... | collective-permute-start | bytes 20 | tf_op jit(solution)/shard_map/ppermute | solution.py:14
  54.6 21.0 %collective-permute-start.5 = (bf16[1,128,256]{2,1,0:T(8,128)(2,1)S(1)}, bf16[1,128,256]{2,1,0:T(8,128)(2,1)S(1)}, u32[]{:S(2)}, u32[]{:S(2)}) collective-permute-start(bf16[1,128,256]{2,1,0:T(8,128)(2,1)S(1)} %get-tuple-element.86), channel_id=1, source_target_pairs={{4,0},{8,4},{12,8},{16,12},{20,16},{24,20},{28,24},{5,1},{9,5},{13... | collective-permute-start | bytes 196616 | tf_op jit(solution)/shard_map/ppermute | solution.py:14
  56.6 3.9 %collective-permute-start.4 = (s32[1]{0:T(128)}, s32[1]{0:T(128)}, u32[]{:S(2)}, u32[]{:S(2)}) collective-permute-start(s32[1]{0:T(128)} %bitcast.25), channel_id=1, source_target_pairs={{4,0},{8,4},{12,8},{16,12},{20,16},{24,20},{28,24},{5,1},{9,5},{13... | collective-permute-start | bytes 20 | tf_op jit(solution)/shard_map/ppermute | solution.py:14
  60.4 5.9 %collective-permute-start.2 = (s32[1]{0:T(128)}, s32[1]{0:T(128)}, u32[]{:S(2)}, u32[]{:S(2)}) collective-permute-start(s32[1]{0:T(128)} %bitcast.17), channel_id=1, source_target_pairs={{8,0},{12,4},{16,8},{20,12},{24,16},{28,20},{9,1},{13,5},{17,9},{2... | collective-permute-start | bytes 20 | tf_op jit(solution)/shard_map/ppermute | solution.py:14
  66.3 5.8 %collective-permute-start = (s32[1]{0:T(128)}, s32[1]{0:T(128)}, u32[]{:S(2)}, u32[]{:S(2)}) collective-permute-start(s32[1]{0:T(128)} %bitcast.9), channel_id=1, source_target_pairs={{12,0},{16,4},{20,8},{24,12},{28,16},{13,1},{17,5},{21,9},{25,13},... | collective-permute-start | bytes 20 | tf_op jit(solution)/shard_map/ppermute | solution.py:14
  72.2 7.3 %collective-permute-start.3 = (bf16[1,128,256]{2,1,0:T(8,128)(2,1)S(1)}, bf16[1,128,256]{2,1,0:T(8,128)(2,1)S(1)}, u32[]{:S(2)}, u32[]{:S(2)}) collective-permute-start(bf16[1,128,256]{2,1,0:T(8,128)(2,1)S(1)} %get-tuple-element.87), channel_id=1, source_target_pairs={{8,0},{12,4},{16,8},{20,12},{24,16},{28,20},{9,1},{13,5},{17,9},{2... | collective-permute-start | bytes 196616 | tf_op jit(solution)/shard_map/ppermute | solution.py:14
  74.1 7.3 %collective-permute-start.1 = (bf16[1,128,256]{2,1,0:T(8,128)(2,1)S(1)}, bf16[1,128,256]{2,1,0:T(8,128)(2,1)S(1)}, u32[]{:S(2)}, u32[]{:S(2)}) collective-permute-start(bf16[1,128,256]{2,1,0:T(8,128)(2,1)S(1)} %get-tuple-element.88), channel_id=1, source_target_pairs={{12,0},{16,4},{20,8},{24,12},{28,16},{13,1},{17,5},{21,9},{25,13},... | collective-permute-start | bytes 196616 | tf_op jit(solution)/shard_map/ppermute | solution.py:14
Sparse Core Ops, SparseCore 0:
  8.9 83.4 all-gather.2
  111.8 25.7 reduce-scatter.1
